TPU v7x, 32 devices: a whole 2x2x4 slice. The times are simulated.
32 devices in a mesh: member: 4 (over y, x), space: 8 (over z, core).
Axes of the slice: x: 2, y: 2, z: 4, core: 2. Of those that a mesh axis runs over, the one named last changes fastest.
Arguments:
- ensemble_prediction: bfloat16 [4, 300, 128, 128], P('member', None, 'space'), may hold values from -6 to 6
- observed_analysis: bfloat16 [300, 128, 128], P(None, 'space'), may hold values from -6 to 6
- validity_flags: int32 [2, 128, 128], P(None, 'space'), may hold values from 0 to 1, as said below
Outputs:
- point_score: float32 [300, 128, 128], P(None, 'space')
- channel_loss: float32 [300], replicated
Inputs may be any that keep to these rules, and one draw needn't show every extreme that they name: `validity_flags`: 0 or 1 for each point and group; every point of latitude row 11 is valid in both groups.
All inputs are finite; a program needn't handle non-finite values.
Results may differ from a plain program's by a relative error of at most 0.0003.
Values may be sent and summed in bfloat16 or wider, within the bound.
A program may use at most 64 MiB of HBM per device.

v0:
```python
import jax
import jax.numpy as jnp
from jax import lax
from jax.sharding import PartitionSpec as P

VARIABLE_NUMBER = 300
ATMOS = 180
TILE_SITES = 128
LON = 720
ROWS = 360


def per_channel(values):
    is_ocean = jnp.arange(VARIABLE_NUMBER, dtype=jnp.int32) >= ATMOS
    return jnp.where(is_ocean, values[1], values[0])


def shards(ensemble_prediction, observed_analysis, validity_flags):
    blocks_here = observed_analysis.shape[1]
    realization_entries = lax.axis_size("member")
    lat_rows = min(ROWS, blocks_here * lax.axis_size("space") * TILE_SITES // LON)
    first_point = lax.axis_index("space") * (blocks_here * TILE_SITES)
    position = first_point + jnp.arange(blocks_here * TILE_SITES, dtype=jnp.int32).reshape(
        blocks_here, TILE_SITES
    )
    inside = (position < lat_rows * LON).astype(jnp.float32)
    lat_row = (position // LON).astype(jnp.float32)
    cosine = jnp.cos(jnp.pi * ((lat_row + 0.5) / lat_rows - 0.5))
    valid = inside[None] * (validity_flags > 0).astype(jnp.float32)
    weight = cosine[None] * valid
    local_area = jnp.sum(weight, axis=(1, 2))
    local_count = jnp.sum(valid, axis=(1, 2))
    is_ocean = jnp.arange(VARIABLE_NUMBER, dtype=jnp.int32) >= ATMOS
    weight_chan = jnp.where(is_ocean[:, None, None], weight[1][None], weight[0][None])
    coeff = (1.0 - 0.05 / realization_entries) / (
        2.0 * realization_entries * (realization_entries - 1)
    )
    gathered = lax.all_to_all(
        ensemble_prediction, "member", split_axis=2, concat_axis=0, tiled=True
    )
    share = blocks_here // realization_entries
    first_block = lax.axis_index("member") * share
    target_part = lax.dynamic_slice_in_dim(observed_analysis, first_block, share, 1).astype(
        jnp.float32
    )
    accuracy_component = jnp.zeros(target_part.shape, jnp.float32)
    dispersion_component = jnp.zeros(target_part.shape, jnp.float32)
    for leading_realization in range(realization_entries):
        lead = gathered[leading_realization].astype(jnp.float32)
        accuracy_component = accuracy_component + jnp.abs(lead - target_part)
        for trailing_realization in range(leading_realization + 1, realization_entries):
            dispersion_component = dispersion_component + jnp.abs(
                lead - gathered[trailing_realization].astype(jnp.float32)
            )
    partial_crps = accuracy_component / realization_entries - coeff * (2.0 * dispersion_component)
    crps = lax.all_gather(partial_crps, "member", axis=1, tiled=True)
    area_sum, count = lax.psum((local_area, local_count), "space")
    scale_chan = per_channel(count / area_sum)
    point_score = crps * weight_chan * scale_chan[:, None, None]
    score_sums = lax.psum(jnp.sum(point_score, axis=(1, 2)), "space")
    channel_loss = score_sums / per_channel(count)
    return (point_score, channel_loss)


def solution(mesh):
    in_specs = (P("member", None, "space", None), P(None, "space", None), P(None, "space", None))
    out_specs = (P(None, "space", None), P())
    return jax.shard_map(shards, mesh=mesh, in_specs=in_specs, out_specs=out_specs, check_vma=False)
```

profile of v0, /device:TPU:0, one launch (start us, length us, event | category | flops | bytes accessed | tf_op | source)
XLA Modules:
  0.0 100.8 jit_solution(2808371847547564155)
XLA Ops:
  7.2 0.0 copy-start
  7.2 2.7 %copy.11 = bf16[1,300,16,128]{3,1,0,2:T(8,128)(2,1)} copy(bf16[1,300,16,128]{3,2,1,0:T(8,128)(2,1)} %param.3) | data formatting | bytes 2457600 | tf_op args[0]
  9.9 0.0 copy-start.1
  9.9 5.3 %all-to-all-start = ((bf16[1,300,16,128]{3,1,0,2:T(8,128)(2,1)}), bf16[1,300,16,128]{3,1,0,2:T(8,128)(2,1)S(1)}, u32[]{:S(2)}, u32[]{:S(2)}) async-start(bf16[1,300,16,128]{3,1,0,2:T(8,128)(2,1)} %copy.11), calls=%async_computation | async-start | bytes 2490368 | tf_op jit(solution)/shard_map/all_to_all | solution.py:38
  15.2 0.0 all-gather.2.cloned.1.call-start
  15.2 0.0 copy-done
  15.2 0.2 constant_dynamic-slice_fusion
  15.4 15.6 %all-to-all-done = bf16[1,300,16,128]{3,1,0,2:T(8,128)(2,1)S(1)} async-done(((bf16[1,300,16,128]{3,1,0,2:T(8,128)(2,1)}), bf16[1,300,16,128]{3,1,0,2:T(8,128)(2,1)S(1)}, u32[]{:S(2)}, u32[]{:S(2)}) %all-to-all-start) | async-done | bytes 1228832 | tf_op jit(solution)/shard_map/all_to_all | solution.py:38
  31.0 1.6 %fusion.5 = f32[300,4,128]{2,0,1:T(8,128)} fusion(bf16[4,1,300,4,128]{4,2,3,0,1:T(8,128)(2,1)S(1)} %bitcast.33, bf16[4,1,300,4,128]{4,2,3,1,0:T(8,128)(2,1)S(1)} %bitcast.34, bf16[300,4,128]{2,1,0:T(4,128)(2,1)S(1)} %constant_dynamic-slice_fusion), kind=kLoop, calls=%fused_computation.16 | loop fusion | flops 5529600 | bytes 2150400 | tf_op jit(solution)/shard_map/sub | solution.py:55
  32.5 0.0 all-gather.2.cloned.1.call-update
  32.6 0.1 fusion.26
  32.7 0.0 copy-done.1
  32.7 0.1 fusion.31
  32.8 0.1 select_reduce_fusion
  32.9 15.9 %all-reduce = (f32[2]{0:T(128)S(1)}, f32[2]{0:T(128)S(1)}) all-reduce(f32[2]{0:T(128)S(1)} %select_reduce_fusion, f32[2]{0:T(128)S(1)} %get-tuple-element.10), channel_id=1, replica_groups=mesh['member'=4,'space'=8] {'space'}, use_global_device_ids=true, to_apply=%region_1.2 | all-reduce | flops 4 | bytes 32 | tf_op jit(solution)/shard_map/psum | solution.py:57
  48.8 0.6 fusion.33
  49.4 1.3 %broadcast_select_fusion = f32[300]{0:T(512)S(1)} fusion(f32[]{:T(128)} %bitcast.16, f32[]{:T(128)} %bitcast.15), kind=kLoop, calls=%fused_computation.56 | loop fusion | flops 600 | bytes 1208 | tf_op jit(solution)/shard_map/jit(_where)/select_n | solution.py:15
  50.7 0.6 fusion.32
  51.3 20.2 %all-gather.2.cloned.1.call-done = f32[300,16,128]{2,0,1:T(8,128)} async-done(((f32[300,4,128]{2,0,1:T(8,128)}), f32[300,16,128]{2,0,1:T(8,128)}) %all-gather.2.cloned.1.call-update) | async-done | bytes 2457616 | tf_op jit(solution)/shard_map/all_gather | solution.py:56
  71.5 2.2 %fusion.30 = (f32[300]{0:T(512)S(1)}, f32[300,16,128]{2,0,1:T(8,128)S(1)}) fusion(f32[300]{0:T(512)S(1)} %broadcast_select_fusion, f32[300,16,128]{2,0,1:T(8,128)} %all-gather.2.cloned.1.call-done, f32[16,128]{1,0:T(8,128)S(1)} %get-tuple-element.14, f32[16,128]{1,0:T(8,128)S(1)} %get-tuple-element.13, pred[300]{0:T(512)(128)(4,1)S(1)} %iota_compare_fusion), kind=kLoop, calls=%fused_computation.58 | loop fusion | flops 2457300 | bytes 4934284 | tf_op jit(solution)/shard_map/reduce_sum | solution.py:60
  73.7 2.2 %copy.16 = f32[300,16,128]{2,1,0:T(8,128)} copy(f32[300,16,128]{2,0,1:T(8,128)S(1)} %get-tuple-element.9) | data formatting | bytes 4915200
  75.9 16.2 %psum.23 = f32[300]{0:T(512)S(1)} all-reduce(f32[300]{0:T(512)S(1)} %get-tuple-element.8), channel_id=1, replica_groups=mesh['member'=4,'space'=8] {'space'}, use_global_device_ids=true, to_apply=%region_5.6 | all-reduce | flops 300 | bytes 2400 | tf_op jit(solution)/shard_map/psum | solution.py:60
  92.1 1.9 %select_divide_fusion = f32[300]{0:T(512)} fusion(f32[300]{0:T(512)S(1)} %psum.23, f32[]{:T(128)} %bitcast.18, f32[]{:T(128)} %bitcast.17), kind=kLoop, calls=%fused_computation.54 | loop fusion | flops 900 | bytes 2408 | tf_op jit(solution)/shard_map/div | solution.py:61
  (4 shorter events, 0.0 us)
Async XLA Ops:
  7.2 8.1 %copy-start = (bf16[300,16,128]{2,1,0:T(8,128)(2,1)S(1)}, bf16[300,16,128]{2,1,0:T(8,128)(2,1)}, u32[]{:S(2)}) copy-start(bf16[300,16,128]{2,1,0:T(8,128)(2,1)} %param.4) | copy-start | bytes 3686404
  9.9 22.7 %copy-start.1 = (s32[2,16,128]{2,1,0:T(8,128)S(1)}, s32[2,16,128]{2,1,0:T(8,128)}, u32[]{:S(2)}) copy-start(s32[2,16,128]{2,1,0:T(8,128)} %param.5) | copy-start | bytes 49156
  9.9 21.1 %all-to-all-start = ((bf16[1,300,16,128]{3,1,0,2:T(8,128)(2,1)}), bf16[1,300,16,128]{3,1,0,2:T(8,128)(2,1)S(1)}, u32[]{:S(2)}, u32[]{:S(2)}) async-start(bf16[1,300,16,128]{3,1,0,2:T(8,128)(2,1)} %copy.11), calls=%async_computation | async-start | bytes 2490368 | tf_op jit(solution)/shard_map/all_to_all | solution.py:38
  15.2 56.2 %all-gather.2.cloned.1.call-start = ((), (), s32[]{:S(2)}) async-start(), calls=%async_computation.1 | async-start | bytes 3112960 | tf_op jit(solution)/shard_map/all_gather | solution.py:56
Sparse Core Ops, SparseCore 0:
  32.7 38.7 all-gather.1
where the time goes:
time: 101 us
  waiting for transfers between devices  35.8 us (35%)
  blocking collectives  32.1 us (32%)
  between operations  14.1 us (14%)
  other arithmetic  7.25 us (7%)
  local copies, waits for them, and re-layouts  6.33 us (6%)
  starting transfers between devices  5.33 us (5%)
    all_gather x1, waiting for transfers between devices, shards(): crps = lax.all_gather(partial_crps, 'member', axis=1, tiled=True)  20.2 us
    psum x1, blocking collectives, shards(): score_sums = lax.psum(jnp.sum(point_score, axis=(1, 2)), 'space')  16.2 us
    psum x1, blocking collectives, shards(): area_sum, count = lax.psum((local_area, local_count), 'space')  15.9 us
    all_to_all x1, waiting for transfers between devices, shards(): lax.all_to_all(ensemble_prediction, 'member', split_axis=2, concat_axis=0...  15.6 us
    all_to_all x1, starting transfers between devices, shards(): lax.all_to_all(ensemble_prediction, 'member', split_axis=2, concat_axis=0...  5.32 us
    unnamed x6, local copies, waits for them, and re-layouts  4.95 us
    reduce_sum x1, other arithmetic, shards(): score_sums = lax.psum(jnp.sum(point_score, axis=(1, 2)), 'space')  2.23 us
  transfers between devices with their start and end apart: 2, of which 2 were waited for; matrix products, arithmetic and copies ran while one was open for 3% of the time, Pallas kernels for 0%

commit v1 on v0

--- a/solution.py
+++ b/solution.py
@@ -53,7 +53,14 @@
                 lead - gathered[trailing_realization].astype(jnp.float32)
             )
     partial_crps = accuracy_component / realization_entries - coeff * (2.0 * dispersion_component)
-    crps = lax.all_gather(partial_crps, "member", axis=1, tiled=True)
+    ring = [partial_crps]
+    for hop in range(3):
+        ring.append(lax.ppermute(ring[-1], "member", [(dev, (dev + 1) % 4) for dev in range(4)]))
+    crps = jnp.roll(
+        jnp.concatenate(ring[::-1], axis=1),
+        (lax.axis_index("member") + 1) * ring[0].shape[1],
+        axis=1,
+    )
     area_sum, count = lax.psum((local_area, local_count), "space")
     scale_chan = per_channel(count / area_sum)
     point_score = crps * weight_chan * scale_chan[:, None, None]

time: 101 us -> 93.8 us (0.929)
  between operations: 14.1 us -> 0.75 us
  waiting for transfers between devices: 35.8 us -> 44.3 us
  blocking collectives: 32.1 us -> 27.8 us
  local copies, waits for them, and re-layouts: 6.33 us -> 9.08 us
  other arithmetic: 7.25 us -> 4.68 us
  starting transfers between devices: 5.33 us -> 6.81 us
    ppermute x0 -> x3, waiting for transfers between devices: none -> 28.7 us  [shards(): lax.ppermute(ring[-1], 'member', [(dev, (dev + 1) % 4) for dev in range(4)])]
    all_gather x1 -> x0, waiting for transfers between devices: 20.2 us -> none  [shards(): crps = lax.all_gather(partial_crps, 'member', axis=1, tiled=True)]
    psum x1, blocking collectives: 16.2 us -> 13.6 us  [shards(): score_sums = lax.psum(jnp.sum(point_score, axis=(1, 2)), 'space')]
    unnamed x6 -> x13, local copies, waits for them, and re-layouts: 4.95 us -> 7.39 us
    psum x1, blocking collectives: 15.9 us -> 14.2 us  [shards(): area_sum, count = lax.psum((local_area, local_count), 'space')]
    reduce_sum x1, other arithmetic: 2.23 us -> 0.53 us  [shards(): score_sums = lax.psum(jnp.sum(point_score, axis=(1, 2)), 'space')]
    ppermute x0 -> x3, starting transfers between devices: none -> 1.62 us  [shards(): lax.ppermute(ring[-1], 'member', [(dev, (dev + 1) % 4) for dev in range(4)])]
  transfers between devices with their start and end apart: 2 -> 4, of which waited for: 2 -> 3; matrix products, arithmetic and copies ran while one was open for 3% -> 3% of each run, Pallas kernels for 0% -> 0%
where the time goes in v1:
time: 93.8 us; the launch traced here: 93.4 us
  waiting for transfers between devices  44.3 us (47%)
  blocking collectives  27.8 us (30%)
  local copies, waits for them, and re-layouts  9.08 us (10%)
  starting transfers between devices  6.81 us (7%)
  other arithmetic  4.68 us (5%)
    ppermute x3, waiting for transfers between devices, shards(): lax.ppermute(ring[-1], 'member', [(dev, (dev + 1) % 4) for dev in range(4)])  28.7 us
    all_to_all x1, waiting for transfers between devices, shards(): lax.all_to_all(ensemble_prediction, 'member', split_axis=2, concat_axis=0...  15.6 us
    psum x1, blocking collectives, shards(): area_sum, count = lax.psum((local_area, local_count), 'space')  14.2 us
    psum x1, blocking collectives, shards(): score_sums = lax.psum(jnp.sum(point_score, axis=(1, 2)), 'space')  13.6 us
    unnamed x13, local copies, waits for them, and re-layouts  7.39 us
    all_to_all x1, starting transfers between devices, shards(): lax.all_to_all(ensemble_prediction, 'member', split_axis=2, concat_axis=0...  5.19 us
  transfers between devices with their start and end apart: 4, of which 3 were waited for; matrix products, arithmetic and copies ran while one was open for 3% of the time, Pallas kernels for 0%

profile of v1, /device:TPU:0, one launch (start us, length us, event | category | flops | bytes accessed | tf_op | source)
XLA Modules:
  0.0 93.4 jit_solution(7731339194148546315)
XLA Ops:
  0.6 0.0 copy-start
  0.6 0.0 copy-start.1
  0.7 2.7 %copy.11 = bf16[1,300,16,128]{3,1,0,2:T(8,128)(2,1)} copy(bf16[1,300,16,128]{3,2,1,0:T(8,128)(2,1)} %param.3) | data formatting | bytes 2457600 | tf_op args[0]
  3.4 5.2 %all-to-all-start = ((bf16[1,300,16,128]{3,1,0,2:T(8,128)(2,1)}), bf16[1,300,16,128]{3,1,0,2:T(8,128)(2,1)S(1)}, u32[]{:S(2)}, u32[]{:S(2)}) async-start(bf16[1,300,16,128]{3,1,0,2:T(8,128)(2,1)} %copy.11), calls=%async_computation | async-start | bytes 2490368 | tf_op jit(solution)/shard_map/all_to_all | solution.py:38
  8.6 0.0 copy-done
  8.6 0.2 constant_dynamic-slice_fusion
  8.8 15.6 %all-to-all-done = bf16[1,300,16,128]{3,1,0,2:T(8,128)(2,1)S(1)} async-done(((bf16[1,300,16,128]{3,1,0,2:T(8,128)(2,1)}), bf16[1,300,16,128]{3,1,0,2:T(8,128)(2,1)S(1)}, u32[]{:S(2)}, u32[]{:S(2)}) %all-to-all-start) | async-done | bytes 1228832 | tf_op jit(solution)/shard_map/all_to_all | solution.py:38
  24.3 0.7 fusion.5
  25.1 0.2 copy.16
  25.3 1.5 %collective-permute-start = (f32[300,4,128]{2,1,0:T(4,128)S(1)}, f32[300,4,128]{2,1,0:T(4,128)S(1)}, u32[]{:S(2)}, u32[]{:S(2)}) collective-permute-start(f32[300,4,128]{2,1,0:T(4,128)S(1)} %copy.16), channel_id=1, source_target_pairs={{0,8},{8,16},{16,24},{24,0},{1,9},{9,17},{17,25},{25,1},{2,10},{10... | collective-permute-start | bytes 1843208 | tf_op jit(solution)/shard_map/ppermute | solution.py:58
  26.8 14.3 %collective-permute-done = f32[300,4,128]{2,1,0:T(4,128)S(1)} collective-permute-done((f32[300,4,128]{2,1,0:T(4,128)S(1)}, f32[300,4,128]{2,1,0:T(4,128)S(1)}, u32[]{:S(2)}, u32[]{:S(2)}) %collective-permute-start) | collective-permute-done | bytes 614432 | tf_op jit(solution)/shard_map/ppermute | solution.py:58
  41.1 0.1 collective-permute-start.1
  41.2 0.1 fusion.26
  41.3 0.0 copy-done.1
  41.3 0.1 fusion.31
  41.4 0.1 select_reduce_fusion
  41.5 14.4 %collective-permute-done.1 = f32[300,4,128]{2,1,0:T(4,128)S(1)} collective-permute-done((f32[300,4,128]{2,1,0:T(4,128)S(1)}, f32[300,4,128]{2,1,0:T(4,128)S(1)}, u32[]{:S(2)}, u32[]{:S(2)}) %collective-permute-start.1) | collective-permute-done | bytes 614432 | tf_op jit(solution)/shard_map/ppermute | solution.py:58
  56.0 0.0 collective-permute-start.2
  56.0 14.2 %all-reduce = (f32[2]{0:T(128)S(1)}, f32[2]{0:T(128)S(1)}) all-reduce(f32[2]{0:T(128)S(1)} %select_reduce_fusion, f32[2]{0:T(128)S(1)} %get-tuple-element.10), channel_id=1, replica_groups=mesh['member'=4,'space'=8] {'space'}, use_global_device_ids=true, to_apply=%region_1.2 | all-reduce | flops 4 | bytes 32 | tf_op jit(solution)/shard_map/psum | solution.py:64
  70.2 0.6 fusion.33
  70.8 1.3 %broadcast_select_fusion = f32[300]{0:T(512)S(1)} fusion(f32[]{:T(128)} %bitcast.16, f32[]{:T(128)} %bitcast.15), kind=kLoop, calls=%fused_computation.64 | loop fusion | flops 600 | bytes 1208 | tf_op jit(solution)/shard_map/jit(_where)/select_n | solution.py:15
  72.1 0.6 fusion.32
  72.7 0.0 collective-permute-done.2
  72.7 1.1 %copy_dynamic-update-slice_fusion.4 = f32[300,32,128]{2,0,1:T(8,128)S(1)} fusion(f32[300,4,128]{2,1,0:T(4,128)} %collective-permute-done.2), kind=kLoop, calls=%fused_computation.36 | loop fusion | bytes 1236992
  74.0 1.1 %copy_dynamic-update-slice_fusion.5 = f32[300,32,128]{2,0,1:T(8,128)S(1)} fusion(f32[300,32,128]{2,0,1:T(8,128)S(1)} %constant_dynamic-update-slice_fusion.1, f32[300,4,128]{2,1,0:T(4,128)} %collective-permute-done.2), kind=kLoop, calls=%fused_computation.37 | loop fusion | bytes 1236992
  75.3 0.5 fusion.30
  75.8 2.2 %copy.23 = f32[300,16,128]{2,1,0:T(8,128)} copy(f32[300,16,128]{2,0,1:T(8,128)S(1)} %get-tuple-element.9) | data formatting | bytes 4915200
  78.0 13.6 %psum.23 = f32[300]{0:T(512)S(1)} all-reduce(f32[300]{0:T(512)S(1)} %get-tuple-element.8), channel_id=1, replica_groups=mesh['member'=4,'space'=8] {'space'}, use_global_device_ids=true, to_apply=%region_5.6 | all-reduce | flops 300 | bytes 2400 | tf_op jit(solution)/shard_map/psum | solution.py:67
  91.6 1.8 %select_divide_fusion = f32[300]{0:T(512)} fusion(f32[300]{0:T(512)S(1)} %psum.23, f32[]{:T(128)} %bitcast.18, f32[]{:T(128)} %bitcast.17), kind=kLoop, calls=%fused_computation.62 | loop fusion | flops 900 | bytes 2408 | tf_op jit(solution)/shard_map/div | solution.py:68
  (10 shorter events, 0.3 us)
Async XLA Ops:
  0.6 8.0 %copy-start = (bf16[300,16,128]{2,1,0:T(8,128)(2,1)S(1)}, bf16[300,16,128]{2,1,0:T(8,128)(2,1)}, u32[]{:S(2)}) copy-start(bf16[300,16,128]{2,1,0:T(8,128)(2,1)} %param.4) | copy-start | bytes 3686404
  0.6 40.7 %copy-start.1 = (s32[2,16,128]{2,1,0:T(8,128)S(1)}, s32[2,16,128]{2,1,0:T(8,128)}, u32[]{:S(2)}) copy-start(s32[2,16,128]{2,1,0:T(8,128)} %param.5) | copy-start | bytes 49156
  3.4 20.9 %all-to-all-start = ((bf16[1,300,16,128]{3,1,0,2:T(8,128)(2,1)}), bf16[1,300,16,128]{3,1,0,2:T(8,128)(2,1)S(1)}, u32[]{:S(2)}, u32[]{:S(2)}) async-start(bf16[1,300,16,128]{3,1,0,2:T(8,128)(2,1)} %copy.11), calls=%async_computation | async-start | bytes 2490368 | tf_op jit(solution)/shard_map/all_to_all | solution.py:38
  25.3 15.8 %collective-permute-start = (f32[300,4,128]{2,1,0:T(4,128)S(1)}, f32[300,4,128]{2,1,0:T(4,128)S(1)}, u32[]{:S(2)}, u32[]{:S(2)}) collective-permute-start(f32[300,4,128]{2,1,0:T(4,128)S(1)} %copy.16), channel_id=1, source_target_pairs={{0,8},{8,16},{16,24},{24,0},{1,9},{9,17},{17,25},{25,1},{2,10},{10... | collective-permute-start | bytes 1843208 | tf_op jit(solution)/shard_map/ppermute | solution.py:58
  41.1 14.9 %collective-permute-start.1 = (f32[300,4,128]{2,1,0:T(4,128)S(1)}, f32[300,4,128]{2,1,0:T(4,128)S(1)}, u32[]{:S(2)}, u32[]{:S(2)}) collective-permute-start(f32[300,4,128]{2,1,0:T(4,128)S(1)} %collective-permute-done), channel_id=1, source_target_pairs={{0,8},{8,16},{16,24},{24,0},{1,9},{9,17},{17,25},{25,1},{2,10},{10... | collective-permute-start | bytes 1843208 | tf_op jit(solution)/shard_map/ppermute | solution.py:58
  56.0 16.8 %collective-permute-start.2 = (f32[300,4,128]{2,1,0:T(4,128)S(1)}, f32[300,4,128]{2,1,0:T(4,128)}, u32[]{:S(2)}, u32[]{:S(2)}) collective-permute-start(f32[300,4,128]{2,1,0:T(4,128)S(1)} %collective-permute-done.1), channel_id=1, source_target_pairs={{0,8},{8,16},{16,24},{24,0},{1,9},{9,17},{17,25},{25,1},{2,10},{10... | collective-permute-start | bytes 1843208 | tf_op jit(solution)/shard_map/ppermute | solution.py:58

commit v2 on v0

--- a/solution.py
+++ b/solution.py
@@ -57,7 +57,7 @@
     area_sum, count = lax.psum((local_area, local_count), "space")
     scale_chan = per_channel(count / area_sum)
     point_score = crps * weight_chan * scale_chan[:, None, None]
-    score_sums = lax.psum(jnp.sum(point_score, axis=(1, 2)), "space")
+    score_sums = jnp.sum(lax.all_gather(jnp.sum(point_score, axis=(1, 2)), "space"), axis=0)
     channel_loss = score_sums / per_channel(count)
     return (point_score, channel_loss)
 

time: 101 us -> 114 us (1.13)
  blocking collectives: 32.1 us -> 44.3 us
  waiting for transfers between devices: 35.8 us -> 34.4 us
    unnamed x0 -> x1, blocking collectives: none -> 28.3 us
    psum x1 -> x0, blocking collectives: 16.2 us -> none  [shards(): score_sums = lax.psum(jnp.sum(point_score, axis=(1, 2)), 'space')]
    all_gather x1, waiting for transfers between devices: 20.2 us -> 18.8 us  [shards(): crps = lax.all_gather(partial_crps, 'member', axis=1, tiled=True)]
    unnamed x6 -> x11, local copies, waits for them, and re-layouts: 4.95 us -> 5.72 us
where the time goes in v2:
time: 114 us; the launch traced here: 113 us
  blocking collectives  44.3 us (39%)
  waiting for transfers between devices  34.4 us (30%)
  between operations  14.7 us (13%)
  other arithmetic  7.34 us (6%)
  local copies, waits for them, and re-layouts  7.23 us (6%)
  starting transfers between devices  5.33 us (5%)
    unnamed x1, blocking collectives  28.3 us
    all_gather x1, waiting for transfers between devices, shards(): crps = lax.all_gather(partial_crps, 'member', axis=1, tiled=True)  18.8 us
    psum x1, blocking collectives, shards(): area_sum, count = lax.psum((local_area, local_count), 'space')  15.9 us
    all_to_all x1, waiting for transfers between devices, shards(): lax.all_to_all(ensemble_prediction, 'member', split_axis=2, concat_axis=0...  15.6 us
    unnamed x11, local copies, waits for them, and re-layouts  5.72 us
    all_to_all x1, starting transfers between devices, shards(): lax.all_to_all(ensemble_prediction, 'member', split_axis=2, concat_axis=0...  5.32 us
  transfers between devices with their start and end apart: 2, of which 2 were waited for; matrix products, arithmetic and copies ran while one was open for 3% of the time, Pallas kernels for 0%

profile of v2, /device:TPU:0, one launch (start us, length us, event | category | flops | bytes accessed | tf_op | source)
XLA Modules:
  0.0 113.3 jit_solution(11325130001480963625)
XLA Ops:
  7.2 0.0 copy-start
  7.2 2.7 %copy.17 = bf16[1,300,16,128]{3,1,0,2:T(8,128)(2,1)} copy(bf16[1,300,16,128]{3,2,1,0:T(8,128)(2,1)} %param.3) | data formatting | bytes 2457600 | tf_op args[0]
  9.9 0.0 copy-start.1
  9.9 0.0 copy-start.2
  9.9 5.3 %all-to-all-start = ((bf16[1,300,16,128]{3,1,0,2:T(8,128)(2,1)}), bf16[1,300,16,128]{3,1,0,2:T(8,128)(2,1)S(1)}, u32[]{:S(2)}, u32[]{:S(2)}) async-start(bf16[1,300,16,128]{3,1,0,2:T(8,128)(2,1)} %copy.17), calls=%async_computation | async-start | bytes 2490368 | tf_op jit(solution)/shard_map/all_to_all | solution.py:38
  15.2 0.0 all-gather.3.cloned.1.call-start
  15.2 0.0 copy-done
  15.2 0.2 constant_dynamic-slice_fusion
  15.4 15.6 %all-to-all-done = bf16[1,300,16,128]{3,1,0,2:T(8,128)(2,1)S(1)} async-done(((bf16[1,300,16,128]{3,1,0,2:T(8,128)(2,1)}), bf16[1,300,16,128]{3,1,0,2:T(8,128)(2,1)S(1)}, u32[]{:S(2)}, u32[]{:S(2)}) %all-to-all-start) | async-done | bytes 1228832 | tf_op jit(solution)/shard_map/all_to_all | solution.py:38
  31.0 1.6 %fusion.5 = f32[300,4,128]{2,0,1:T(8,128)} fusion(bf16[4,1,300,4,128]{4,2,3,0,1:T(8,128)(2,1)S(1)} %bitcast.34, bf16[4,1,300,4,128]{4,2,3,1,0:T(8,128)(2,1)S(1)} %bitcast.35, bf16[300,4,128]{2,1,0:T(4,128)(2,1)S(1)} %constant_dynamic-slice_fusion), kind=kLoop, calls=%fused_computation.16 | loop fusion | flops 5529600 | bytes 2150400 | tf_op jit(solution)/shard_map/sub | solution.py:55
  32.5 0.0 all-gather.3.cloned.1.call-update
  32.6 0.1 fusion.26
  32.7 0.0 copy-done.1
  32.7 0.1 fusion.31
  32.8 0.1 select_reduce_fusion
  32.9 15.9 %all-reduce.1 = (f32[2]{0:T(128)S(1)}, f32[2]{0:T(128)S(1)}) all-reduce(f32[2]{0:T(128)S(1)} %select_reduce_fusion, f32[2]{0:T(128)S(1)} %get-tuple-element.12), channel_id=1, replica_groups=mesh['member'=4,'space'=8] {'space'}, use_global_device_ids=true, to_apply=%region_1.2 | all-reduce | flops 4 | bytes 32 | tf_op jit(solution)/shard_map/psum | solution.py:57
  48.8 0.0 copy-done.2
  48.8 0.6 dynamic-slice
  50.0 0.6 fusion.33
  50.6 1.3 %broadcast_select_fusion = f32[300]{0:T(512)S(1)} fusion(f32[]{:T(128)} %bitcast.16, f32[]{:T(128)} %bitcast.15), kind=kLoop, calls=%fused_computation.56 | loop fusion | flops 600 | bytes 1208 | tf_op jit(solution)/shard_map/jit(_where)/select_n | solution.py:15
  52.0 0.7 fusion.32
  52.7 18.8 %all-gather.3.cloned.1.call-done = f32[300,16,128]{2,0,1:T(8,128)} async-done(((f32[300,4,128]{2,0,1:T(8,128)}), f32[300,16,128]{2,0,1:T(8,128)}) %all-gather.3.cloned.1.call-update) | async-done | bytes 2457616 | tf_op jit(solution)/shard_map/all_gather | solution.py:56
  71.5 2.2 %fusion.30 = (f32[300]{0:T(512)S(1)}, f32[300,16,128]{2,0,1:T(8,128)S(1)}) fusion(f32[300]{0:T(512)S(1)} %broadcast_select_fusion, f32[300,16,128]{2,0,1:T(8,128)} %all-gather.3.cloned.1.call-done, f32[16,128]{1,0:T(8,128)S(1)} %get-tuple-element.16, f32[16,128]{1,0:T(8,128)S(1)} %get-tuple-element.15, pred[300]{0:T(512)(128)(4,1)S(1)} %iota_compare_fusion), kind=kLoop, calls=%fused_computation.58 | loop fusion | flops 2457300 | bytes 4934284 | tf_op jit(solution)/shard_map/reduce_sum | solution.py:60
  73.7 2.2 %copy.22 = f32[300,16,128]{2,1,0:T(8,128)} copy(f32[300,16,128]{2,0,1:T(8,128)S(1)} %get-tuple-element.11) | data formatting | bytes 4915200
  75.9 0.2 dynamic-update-slice
  76.1 28.3 %all-reduce = f32[2400]{0:T(1024)S(1)} all-reduce(f32[2400]{0:T(1024)S(1)} %dynamic-update-slice), channel_id=2, replica_groups=mesh['member'=4,'space'=8] {'space'}, use_global_device_ids=true, to_apply=%add | all-reduce | flops 2400 | bytes 19200
  104.4 0.1 reshape.70
  104.5 1.9 %select_divide_fusion = f32[300]{0:T(512)} fusion(f32[300]{0:T(512)S(1)} %reduce_sum.39, f32[]{:T(128)} %bitcast.19, f32[]{:T(128)} %bitcast.18), kind=kLoop, calls=%fused_computation.54 | loop fusion | flops 900 | bytes 2408 | tf_op jit(solution)/shard_map/div | solution.py:61
  (6 shorter events, 0.0 us)
Async XLA Ops:
  7.2 8.1 %copy-start = (bf16[300,16,128]{2,1,0:T(8,128)(2,1)S(1)}, bf16[300,16,128]{2,1,0:T(8,128)(2,1)}, u32[]{:S(2)}) copy-start(bf16[300,16,128]{2,1,0:T(8,128)(2,1)} %param.4) | copy-start | bytes 3686404
  9.9 22.7 %copy-start.1 = (s32[2,16,128]{2,1,0:T(8,128)S(1)}, s32[2,16,128]{2,1,0:T(8,128)}, u32[]{:S(2)}) copy-start(s32[2,16,128]{2,1,0:T(8,128)} %param.5) | copy-start | bytes 49156
  9.9 38.9 %copy-start.2 = (u32[32]{0:T(128)S(1)}, u32[32]{0:T(128)}, u32[]{:S(2)}) copy-start(u32[32]{0:T(128)} %constant.55) | copy-start | bytes 388
  9.9 21.1 %all-to-all-start = ((bf16[1,300,16,128]{3,1,0,2:T(8,128)(2,1)}), bf16[1,300,16,128]{3,1,0,2:T(8,128)(2,1)S(1)}, u32[]{:S(2)}, u32[]{:S(2)}) async-start(bf16[1,300,16,128]{3,1,0,2:T(8,128)(2,1)} %copy.17), calls=%async_computation | async-start | bytes 2490368 | tf_op jit(solution)/shard_map/all_to_all | solution.py:38
  15.2 56.2 %all-gather.3.cloned.1.call-start = ((), (), s32[]{:S(2)}) async-start(), calls=%async_computation.1 | async-start | bytes 3112960 | tf_op jit(solution)/shard_map/all_gather | solution.py:56
Sparse Core Ops, SparseCore 0:
  32.7 38.7 all-gather.2
